TPU v7x, 32 devices: a whole 2x2x4 slice. The times are simulated.
32 devices in a mesh: aa: 2 (over core), ba: 16 (over z, y, x).
Axes of the slice: x: 2, y: 2, z: 4, core: 2. Of those that a mesh axis runs over, the one named last changes fastest.
Arguments:
- queries: bfloat16 [2, 16, 192, 1024], P('aa', 'ba'), may hold values from -6 to 6
- key_rows: bfloat16 [2, 16, 192, 1024], P('aa', 'ba'), may hold values from -6 to 6
- value_rows: bfloat16 [2, 16, 192, 1024], P('aa', 'ba'), may hold values from -6 to 6
- out_proj: bfloat16 [2, 1024, 1024], P('aa', 'ba'), may hold values from -0.1875 to 0.1875
- scale_ids: int32 [16, 192], P('ba'), may hold values from 0 to 7, never falling along the last dimension, each value on 1 to 64 neighbouring positions
- residual_in: bfloat16 [16, 192, 1024], P('ba'), may hold values from -4 to 4
- cotangent: bfloat16 [16, 192, 1024], P('ba'), may hold values from -6 to 6
Outputs:
- residual_out: bfloat16 [2, 16, 192, 1024], P('aa', 'ba')
- grad_query: bfloat16 [2, 16, 192, 1024], P('aa', 'ba')
- grad_key: bfloat16 [2, 16, 192, 1024], P('aa', 'ba')
- grad_value: bfloat16 [2, 16, 192, 1024], P('aa', 'ba')
- grad_proj: float32 [2, 1024, 1024], P('aa', 'ba')
Inputs may be any that keep to these rules, and one draw needn't show every extreme that they name: `scale_ids`: for each image the scale ids never fall along the tokens; every scale from 0 to 7 is present, with 1 to 64 tokens.
All inputs are finite; a program needn't handle non-finite values.
Results may differ from a plain program's by a relative error of at most 0.0086.
Values may be sent and summed in bfloat16 or wider, within the bound.
A program may use at most 64 MiB of HBM per device.

v0:
```python
import functools

import jax
import jax.numpy as jnp
from jax import lax
from jax.experimental import pallas as pl
from jax.experimental.pallas import tpu as pltpu
from jax.sharding import PartitionSpec as P

HD = 64


def passed_along(value, axis, by):
    devices = lax.axis_size(axis)
    pairs = [(i, i + by) for i in range(devices) if 0 <= i + by < devices]
    return lax.ppermute(value, axis, pairs)


def local(queries, key_rows, value_rows, out_proj, scale_ids, residual_in, cotangent):
    images = queries.shape[1]
    length = queries.shape[2]
    inner_width = queries.shape[3]
    head_count = inner_width // HD
    res_width = residual_in.shape[2]
    flat_rows = images * length
    score_scale = HD ** (-0.5)
    image_weight = 1.0 / (lax.axis_size("ba") * images)
    w_full = lax.all_gather(out_proj, "ba", axis=1, tiled=True)[0]
    visible = scale_ids[:, None, :] <= scale_ids[:, :, None]
    q_heads = queries[0].reshape(images, length, head_count, HD)
    k_heads = key_rows[0].reshape(images, length, head_count, HD)
    v_heads = value_rows[0].reshape(images, length, head_count, HD)
    scores = (
        jnp.einsum("bihd,bjhd->bhij", q_heads, k_heads, preferred_element_type=jnp.float32)
        * score_scale
    )
    scores = jnp.where(visible[:, None], scores, -jnp.inf)
    row_max = jnp.max(scores, axis=-1, keepdims=True)
    lifted = jnp.exp(scores - row_max)
    attn_probs = lifted / jnp.sum(lifted, axis=-1, keepdims=True)
    probs_low = attn_probs.astype(jnp.bfloat16)
    attended = jnp.einsum("bhij,bjhd->bihd", probs_low, v_heads, preferred_element_type=jnp.float32)
    attn_rows = attended.astype(jnp.bfloat16).reshape(flat_rows, inner_width)
    branch = jnp.dot(attn_rows, w_full, preferred_element_type=jnp.float32)

    def relay_step(hop_index, running):
        return branch + passed_along(running, "aa", 1)

    carried = lax.fori_loop(0, lax.axis_size("aa") - 1, relay_step, branch)
    residual_rows = residual_in.reshape(flat_rows, res_width).astype(jnp.float32) + carried
    residual_out = residual_rows.astype(jnp.bfloat16).reshape(images, length, res_width)
    cot_rows = cotangent.reshape(flat_rows, res_width)
    d_attn = lax.dot_general(
        cot_rows, w_full, (((1,), (1,)), ((), ())), preferred_element_type=jnp.float32
    ).astype(jnp.bfloat16)
    product = lax.dot_general(
        attn_rows, cot_rows, (((0,), (0,)), ((), ())), preferred_element_type=jnp.float32
    )
    grad_proj = lax.psum_scatter(product * image_weight, "ba", scatter_dimension=0, tiled=True)
    d_heads = d_attn.reshape(images, length, head_count, HD)
    grad_value = jnp.einsum(
        "bhij,bihd->bjhd", probs_low, d_heads, preferred_element_type=jnp.float32
    )
    d_probs = jnp.einsum("bihd,bjhd->bhij", d_heads, v_heads, preferred_element_type=jnp.float32)
    row_delta = jnp.sum(attn_probs * d_probs, axis=-1, keepdims=True)
    d_scores = (attn_probs * (d_probs - row_delta) * score_scale).astype(jnp.bfloat16)
    grad_query = jnp.einsum(
        "bhij,bjhd->bihd", d_scores, k_heads, preferred_element_type=jnp.float32
    )
    grad_key = jnp.einsum("bhij,bihd->bjhd", d_scores, q_heads, preferred_element_type=jnp.float32)
    return (
        residual_out[None],
        grad_query.reshape(images, length, inner_width).astype(jnp.bfloat16)[None],
        grad_key.reshape(images, length, inner_width).astype(jnp.bfloat16)[None],
        grad_value.reshape(images, length, inner_width).astype(jnp.bfloat16)[None],
        grad_proj[None],
    )

BF = jnp.bfloat16
F32 = jnp.float32
NT = (((1,), (1,)), ((), ()))
PAIR = 2 * HD


def nt(a, b):
    return lax.dot_general(a, b, NT, preferred_element_type=F32)


def mm(a, b):
    return jnp.dot(a, b, preferred_element_type=F32)


def turned(value):
    return value.astype(F32).T


def flipped(z, k):
    out, bit = z, 1
    while bit <= k:
        if k & bit:
            out = out + bit - 2 * bit * ((z // bit) % 2)
        bit *= 2
    return out


def fused(
    planes, weight,
    q_in, k_in, v_in, w_in, ids_in, res_in, cot_in,
    out_ref, gq_ref, gk_ref, gv_ref, gp_ref,
    wbuf, cotg, attg, transit, att_send, att_cols, att_rows, probs, bias, dbuf,
    prod, rs_send, rs_recv, branch, running,
    q_ref, k_ref, v_ref, ids_ref, res_ref, cot_ref, send_sems, recv_sems, load_sems,
):
    length, inner = q_ref.shape
    res_width = cot_ref.shape[1]
    rows = w_in.shape[0]
    half, quarter = length // 2, length // 4
    scale = HD ** (-0.5)
    sections = lax.axis_size("aa")
    a, b = lax.axis_index("aa"), lax.axis_index("ba")
    x, y, z = b % 2, (b // 2) % 2, b // 4
    q = b % 4
    xn, yn = b + 1 - 2 * x, b + 2 - 4 * y
    qx, qy, qd = q + 1 - 2 * x, q + 2 - 4 * y, 3 - q
    zs = [flipped(z, k) for k in range(planes)]

    def there(dest, other=False):
        return {"aa": 1 - a if other else a, "ba": dest}

    def rows_of(start, size, step):
        return pl.ds(pl.multiple_of(start, step), size)

    w_ref = wbuf.at[rows_of(b * rows, rows, rows)]
    loads = [
        pltpu.make_async_copy(src, dst, load_sems.at[i])
        for i, (src, dst) in enumerate((
            (cot_in, cot_ref), (w_in, w_ref), (ids_in, ids_ref), (q_in, q_ref),
            (k_in, k_ref), (v_in, v_ref), (res_in, res_ref),
        ))
    ]
    for load in loads:
        load.start()

    barrier = pltpu.get_barrier_semaphore()
    greeted = [there(xn), there(yn), there(b, True)]
    greeted += [there(b + 4 * (zs[k] - z)) for k in range(1, planes)]
    for device in greeted:
        pl.semaphore_signal(
            barrier, inc=1, device_id=device, device_id_type=pl.DeviceIdType.MESH
        )
    pl.semaphore_wait(barrier, len(greeted))

    count = [0]

    def remote(src, dst, device):
        i = count[0]
        count[0] += 1
        return pltpu.make_async_remote_copy(
            src_ref=src, dst_ref=dst, send_sem=send_sems.at[i], recv_sem=recv_sems.at[i],
            device_id=device, device_id_type=pl.DeviceIdType.MESH,
        )

    def shard(zk, qq, part=None):
        start = (zk * 4 + qq) * rows
        if part is None:
            return wbuf.at[rows_of(start, rows, rows)]
        return wbuf.at[rows_of(start + part * (rows // 2), rows // 2, rows // 2)]

    my_half = rows_of(a * half, half, quarter)
    part_a = rows_of(a * half, quarter, quarter)
    part_b = rows_of(a * half + quarter, quarter, quarter)
    other = there(b, True)
    to_x, to_y = there(xn), there(yn)

    cot_x = remote(cot_ref.at[my_half], cotg.at[0, my_half], to_x)
    cot_y = remote(cot_ref.at[my_half], cotg.at[1, my_half], to_y)
    cot_xo = remote(cotg.at[0, my_half], cotg.at[0, my_half], other)
    cot_yo = remote(cotg.at[1, my_half], cotg.at[1, my_half], other)
    cot_da = remote(cotg.at[0, part_a], cotg.at[2, part_a], to_y)
    cot_db = remote(cotg.at[1, part_b], cotg.at[2, part_b], to_x)
    cot_do = remote(cotg.at[2, my_half], cotg.at[2, my_half], other)
    w_z = [None] + [
        remote(w_ref, shard(z, q), there(b + 4 * (zs[k] - z))) for k in range(1, planes)
    ]
    w_x, w_y, w_a, w_b = [], [], [], []
    for k in range(planes):
        mine = w_ref if k == 0 else shard(zs[k], q)
        w_x.append(remote(mine, shard(zs[k], q), to_x))
        w_y.append(remote(mine, shard(zs[k], q), to_y))
        if k == 1:
            w_d = remote(shard(z, qd), shard(z, qd), there(b + 4 * (zs[1] - z)))
            w_a.append(w_d)
            w_b.append(w_d)
            continue
        w_a.append(remote(shard(zs[k], qx, 0), shard(zs[k], qx, 0), to_y))
        w_b.append(remote(shard(zs[k], qy, 1), shard(zs[k], qy, 1), to_x))
    low, high = pl.ds(0, half), pl.ds(half, half)
    att_x = remote(att_send.at[qx], attg.at[0], to_x)
    att_y = remote(att_send.at[qy], attg.at[1], to_y)
    att_ta = remote(att_send.at[qd, low], transit.at[0], to_x)
    att_tb = remote(att_send.at[qd, high], transit.at[1], to_y)
    att_fa = remote(transit.at[0], attg.at[2, low], to_y)
    att_fb = remote(transit.at[1], attg.at[2, high], to_x)
    rs_z = [None] + [
        remote(
            rs_send.at[rows_of(zs[k] * rows, rows, rows)], rs_recv.at[k - 1],
            there(b + 4 * (zs[k] - z)),
        )
        for k in range(1, planes)
    ]
    relay = remote(branch, running, other)
    started = []

    def go(*copies):
        for copy in copies:
            copy.start()
            started.append(copy)

    loads[0].wait()
    go(cot_x, cot_y)
    loads[1].wait()
    go(w_x[0], w_y[0])
    go(*w_z[1:])
    loads[2].wait()
    seen = jnp.broadcast_to(ids_ref[...].astype(F32), (length, length))
    bias[...] = jnp.where(seen.T <= seen, 0.0, -jnp.inf)
    lane = lax.broadcasted_iota(jnp.int32, (1, PAIR), 1)
    ones = [jnp.where(lane // HD == h, 1.0, 0.0).astype(BF) for h in range(2)]
    scaled = [jnp.where(lane // HD == h, scale, 0.0).astype(BF) for h in range(2)]

    for load in loads[3:]:
        load.wait()

    width = 4 * HD

    def forward(zk, carry):
        unit = rows_of(zk * width, width, width)
        q4, k4 = q_ref[:, unit], k_ref[:, unit]
        v_turned = turned(v_ref[:, unit]).astype(BF)
        spans = [slice(h // 2 * PAIR, (h // 2 + 1) * PAIR) for h in range(4)]
        scores = [
            nt(k4[:, spans[h]] * scaled[h % 2], q4[:, spans[h]]) + bias[...] for h in range(4)
        ]
        shares = []
        for h in range(4):
            lifted = jnp.exp(scores[h] - jnp.max(scores[h], axis=0, keepdims=True))
            shares.append(lifted * (1.0 / jnp.sum(lifted, axis=0, keepdims=True)))
        parts = [mm(v_turned[h * HD:(h + 1) * HD], shares[h].astype(BF)) for h in range(4)]
        for h in range(4):
            att_cols[h, rows_of(zk * HD, HD, HD), :] = parts[h].astype(BF)
            probs[4 * zk + h] = shares[h]
        att_rows[:, unit] = jnp.concatenate(parts, axis=0).T.astype(BF)
        return carry

    lax.fori_loop(0, planes, forward, 0)
    for h in range(4):
        att_send[h] = turned(att_cols[h]).astype(BF)

    cot_x.wait_recv()
    cot_y.wait_recv()
    go(cot_xo, cot_yo)
    go(att_ta, att_tb, att_x, att_y)
    go(cot_da, cot_db)

    def pass_planes(k):
        w_z[k].wait_recv()
        go(w_x[k], w_y[k])

    def pass_diagonal(k):
        w_x[k].wait_recv()
        w_y[k].wait_recv()
        if k != 1:
            go(w_a[k], w_b[k])

    def backward(k, first):
        unit = rows_of(zs[k] * width, width, width)
        dbuf[...] = nt(cot_ref[...], wbuf[unit, :]).astype(BF)
        mine = att_rows[:, unit]

        def add(c, carry):
            tile = rows_of(c * 256, 256, 256)
            term = mm(mine, wbuf[unit, tile])
            branch[:, tile] = term if first else branch[:, tile] + term
            return carry

        lax.fori_loop(0, res_width // 256, add, 0, unroll=True)

    def grads(k):
        unit = rows_of(zs[k] * width, width, width)
        d4, q4, v4 = dbuf[...], q_ref[:, unit], v_ref[:, unit]
        k_turned = turned(k_ref[:, unit]).astype(BF)
        spans = [slice(h // 2 * PAIR, (h // 2 + 1) * PAIR) for h in range(4)]
        d_probs = [nt(v4[:, spans[h]] * ones[h % 2], d4[:, spans[h]]) for h in range(4)]
        d_scores, low = [], []
        for h in range(4):
            share = probs[4 * zs[k] + h]
            delta = jnp.sum(share * d_probs[h], axis=0, keepdims=True)
            d_scores.append((share * (d_probs[h] - delta)).astype(BF))
            low.append(share.astype(BF))
        gv = [mm(low[h], d4[:, spans[h]] * ones[h % 2]) for h in range(4)]
        gk = [mm(d_scores[h], q4[:, spans[h]] * scaled[h % 2]) for h in range(4)]
        gq = [mm(k_turned[h * HD:(h + 1) * HD], d_scores[h]) for h in range(4)]
        gv_ref[:, unit] = jnp.concatenate([gv[0] + gv[1], gv[2] + gv[3]], axis=1).astype(BF)
        gk_ref[:, unit] = jnp.concatenate([gk[0] + gk[1], gk[2] + gk[3]], axis=1).astype(BF)
        gq_ref[:, unit] = (jnp.concatenate(gq, axis=0) * scale).T.astype(BF)

    def last_piece(k):
        w_a[k].wait_recv()
        if k != 1:
            w_b[k].wait_recv()
        if k == 0:
            go(w_d)

    att_ta.wait_recv()
    att_tb.wait_recv()
    go(att_fa, att_fb)
    pass_diagonal(0)
    pass_planes(1)
    cot_da.wait_recv()
    cot_db.wait_recv()
    go(cot_do)
    for k in range(2, planes):
        pass_planes(k)
    last_piece(0)
    backward(0, True)
    for copy in (cot_xo, cot_yo, cot_do, att_x, att_y, att_fa, att_fb):
        copy.wait_recv()

    flat = [turned(attg[i]).astype(BF) for i in range(3)]

    def product(c, carry):
        tile = rows_of(c * 256, 256, 256)
        total = mm(att_cols[q], cot_ref[:, tile])
        for i in range(3):
            total = total + mm(flat[i], cotg[i, :, tile])
        total = total * weight
        prod[:, tile] = total
        rs_send[:, tile] = total.astype(BF)
        return carry

    lax.fori_loop(0, res_width // 256, product, 0)
    pass_diagonal(1)
    go(*rs_z[:0:-1])
    grads(0)
    for k in range(1, planes):
        if k + 1 < planes:
            pass_diagonal(k + 1)
        last_piece(k)
        backward(k, False)
        if k == planes - 1:
            @pl.when(a == 0)
            def _():
                relay.start()
        grads(k)
    total = prod[rows_of(z * rows, rows, rows), :]
    for k in range(1, planes):
        rs_z[k].wait_recv()
        total = total + rs_recv[k - 1].astype(F32)
    gp_ref[...] = total
    base = res_ref[...].astype(F32) + branch[...]

    @pl.when(a == 0)
    def _():
        out_ref[...] = base.astype(BF)
        relay.wait_send()

    @pl.when(a == 1)
    def _():
        relay.wait_recv()
        out_ref[...] = (base + running[...]).astype(BF)

    for copy in started:
        copy.wait_send()


def flush(*refs):
    inward, outward, sems = refs[:5], refs[5:10], refs[10]
    copies = [pltpu.make_async_copy(inward[i], outward[i], sems.at[i]) for i in range(5)]
    for copy in copies:
        copy.start()
    for copy in copies:
        copy.wait()


def fused_local(queries, key_rows, value_rows, out_proj, scale_ids, residual_in, cotangent):
    n = lax.axis_size("ba")
    length, inner = queries.shape[2:]
    res_width = residual_in.shape[2]
    rows = out_proj.shape[1]
    planes = n // 4
    copies = 7 + (planes - 1) + 4 * planes + 6 + (planes - 1) + 1
    heads = inner // HD
    wide = jax.ShapeDtypeStruct((length, inner), BF)
    shapes = [
        jax.ShapeDtypeStruct((length, res_width), BF), wide, wide, wide,
        jax.ShapeDtypeStruct((rows, res_width), F32),
    ]
    outs = pl.pallas_call(
        functools.partial(fused, planes, 1.0 / n),
        out_shape=shapes,
        in_specs=[pl.BlockSpec(memory_space=pltpu.HBM)] * 7,
        out_specs=[pl.BlockSpec(memory_space=pltpu.VMEM)] * 5,
        scratch_shapes=[
            pltpu.VMEM((inner, res_width), BF),
            pltpu.VMEM((3, length, res_width), BF),
            pltpu.VMEM((3, length, planes * rows), BF),
            pltpu.VMEM((2, length // 2, planes * rows), BF),
            pltpu.VMEM((4, length, planes * rows), BF),
            pltpu.VMEM((4, planes * rows, length), BF),
            pltpu.VMEM((length, inner), BF),
            pltpu.VMEM((heads, length, length), F32),
            pltpu.VMEM((length, length), F32),
            pltpu.VMEM((length, 4 * HD), BF),
            pltpu.VMEM((planes * rows, res_width), F32),
            pltpu.VMEM((planes * rows, res_width), BF),
            pltpu.VMEM((planes - 1, rows, res_width), BF),
            pltpu.VMEM((length, res_width), F32),
            pltpu.VMEM((length, res_width), F32),
            pltpu.VMEM((length, inner), BF),
            pltpu.VMEM((length, inner), BF),
            pltpu.VMEM((length, inner), BF),
            pltpu.VMEM((1, length), jnp.int32),
            pltpu.VMEM((length, res_width), BF),
            pltpu.VMEM((length, res_width), BF),
            pltpu.SemaphoreType.DMA((copies,)),
            pltpu.SemaphoreType.DMA((copies,)),
            pltpu.SemaphoreType.DMA((7,)),
        ],
        compiler_params=pltpu.CompilerParams(
            collective_id=0, has_side_effects=True, vmem_limit_bytes=50 * 1024 * 1024
        ),
        name="fused_sections",
    )(*[
        pltpu.with_memory_space_constraint(part, pltpu.HBM)
        for part in (
            queries[0, 0], key_rows[0, 0], value_rows[0, 0], out_proj[0], scale_ids,
            residual_in[0], cotangent[0],
        )
    ])
    outs = pl.pallas_call(
        flush,
        out_shape=shapes,
        in_specs=[pl.BlockSpec(memory_space=pltpu.VMEM)] * 5,
        out_specs=[pl.BlockSpec(memory_space=pltpu.HBM)] * 5,
        scratch_shapes=[pltpu.SemaphoreType.DMA((5,))],
        compiler_params=pltpu.CompilerParams(vmem_limit_bytes=8 * 1024 * 1024),
        name="flush",
    )(*outs)
    return (
        outs[0][None, None], outs[1][None, None], outs[2][None, None], outs[3][None, None],
        outs[4][None],
    )


def body_for(queries, key_rows, value_rows, out_proj, scale_ids, residual_in, cotangent):
    n, sections = lax.axis_size("ba"), lax.axis_size("aa")
    images, length, inner = queries.shape[1:]
    fits = (
        sections == 2 and images == 1 and n in (8, 16, 32)
        and out_proj.shape[1] == HD and length % 64 == 0 and residual_in.shape[2] % 256 == 0
    )
    chosen = fused_local if fits else local
    return chosen(
        queries, key_rows, value_rows, out_proj, scale_ids, residual_in, cotangent
    )


def solution(mesh):
    placed = (
        P("aa", "ba", None, None),
        P("aa", "ba", None, None),
        P("aa", "ba", None, None),
        P("aa", "ba", None),
        P("ba", None),
        P("ba", None, None),
        P("ba", None, None),
    )
    return jax.shard_map(
        body_for,
        mesh=mesh,
        in_specs=placed,
        out_specs=(
            P("aa", "ba", None, None),
            P("aa", "ba", None, None),
            P("aa", "ba", None, None),
            P("aa", "ba", None, None),
            P("aa", "ba", None),
        ),
        check_vma=False,
    )
```

profile of v0, /device:TPU:0, one launch (start us, length us, event | category | flops | bytes accessed | tf_op | source)
XLA Modules:
  0.0 41.2 jit_solution(12046916523359571602)
XLA Ops:
  0.6 39.3 %fused_sections.1 = (bf16[192,1024]{1,0:T(8,128)(2,1)S(1)}, bf16[192,1024]{1,0:T(8,128)(2,1)S(1)}, bf16[192,1024]{1,0:T(8,128)(2,1)S(1)}, bf16[192,1024]{1,0:T(8,128)(2,1)S(1)}, f32[64,1024]{1,0:T(8,128)S(1)}) custom-call(bf16[192,1024]{1,0:T(8,128)(2,1)} %bitcast.11, bf16[192,1024]{1,0:T(8,128)(2,1)} %bitcast.12, bf16[192,1024]{1,0:T(8,128)(2,1)} %bitcast.13, ...), custom_call_target="tpu_custom_call" | custom-call | tf_op jit(solution)/shard_map/fused_sections/pallas_call | solution.py:398
  39.9 1.3 %flush.1 = (bf16[192,1024]{1,0:T(8,128)(2,1)}, bf16[192,1024]{1,0:T(8,128)(2,1)}, bf16[192,1024]{1,0:T(8,128)(2,1)}, bf16[192,1024]{1,0:T(8,128)(2,1)}, f32[64,1024]{1,0:T(8,128)}) custom-call(bf16[192,1024]{1,0:T(8,128)(2,1)S(1)} %get-tuple-element.15.refs_0_, bf16[192,1024]{1,0:T(8,128)(2,1)S(1)} %get-tuple-element.16.refs_1_, ...), custom_call_target="tpu_custom_call" | custom-call | tf_op jit(solution)/shard_map/flush/pallas_call | solution.py:440
where the time goes:
time: 41.3 us; the launch traced here: 41.2 us
  Pallas kernels  40.5 us (98%)
  between operations  0.64 us (2%)
    pallas_call x1, Pallas kernels, fused_local(): pl.pallas_call(functools.partial(fused, planes, 1.0 / n), out_shape=shape...  39.3 us
    pallas_call x1, Pallas kernels, fused_local(): pl.pallas_call(flush, out_shape=shapes, in_specs=[pl.BlockSpec(memory_spa...  1.27 us

commit v1 on v0

--- a/solution.py
+++ b/solution.py
@@ -109,7 +109,7 @@
     out_ref, gq_ref, gk_ref, gv_ref, gp_ref,
     wbuf, cotg, attg, transit, att_send, att_cols, att_rows, probs, bias, dbuf,
     prod, rs_send, rs_recv, branch, running,
-    q_ref, k_ref, v_ref, ids_ref, res_ref, cot_ref, send_sems, recv_sems, load_sems,
+    q_ref, k_ref, v_ref, ids_ref, res_ref, cot_ref, send_sems, recv_sems, load_sems, above_sems,
 ):
     length, inner = q_ref.shape
     res_width = cot_ref.shape[1]
@@ -142,13 +142,24 @@
         load.start()
 
     barrier = pltpu.get_barrier_semaphore()
-    greeted = [there(xn), there(yn), there(b, True)]
-    greeted += [there(b + 4 * (zs[k] - z)) for k in range(1, planes)]
-    for device in greeted:
+    columns = [there(b + 4 * (zs[k] - z)) for k in range(planes)]
+
+    def greet(semaphore, device):
         pl.semaphore_signal(
-            barrier, inc=1, device_id=device, device_id_type=pl.DeviceIdType.MESH
+            semaphore, inc=1, device_id=device, device_id_type=pl.DeviceIdType.MESH
         )
-    pl.semaphore_wait(barrier, len(greeted))
+
+    for device in (there(xn), there(yn), there(b, True)):
+        greet(barrier, device)
+    for k in range(1, planes):
+        @pl.when(zs[k] > z)
+        def _(k=k):
+            greet(barrier, columns[k])
+    pl.semaphore_wait(barrier, 3 + z)
+    for k in range(1, planes):
+        @pl.when(zs[k] < z)
+        def _(k=k):
+            greet(above_sems.at[k], columns[k])
 
     count = [0]
 
@@ -220,7 +231,17 @@
     go(cot_x, cot_y)
     loads[1].wait()
     go(w_x[0], w_y[0])
-    go(*w_z[1:])
+
+    def to_planes(above):
+        for k in range(1, planes):
+            @pl.when(zs[k] > z if above else zs[k] < z)
+            def _(k=k):
+                if above:
+                    pl.semaphore_wait(above_sems.at[k], 1)
+                w_z[k].start()
+
+    to_planes(False)
+    started.extend(w_z[1:])
     loads[2].wait()
     seen = jnp.broadcast_to(ids_ref[...].astype(F32), (length, length))
     bias[...] = jnp.where(seen.T <= seen, 0.0, -jnp.inf)
@@ -252,7 +273,9 @@
         att_rows[:, unit] = jnp.concatenate(parts, axis=0).T.astype(BF)
         return carry
 
-    lax.fori_loop(0, planes, forward, 0)
+    lax.fori_loop(0, planes // 2, forward, 0)
+    to_planes(True)
+    lax.fori_loop(planes // 2, planes, forward, 0)
     for h in range(4):
         att_send[h] = turned(att_cols[h]).astype(BF)
 
@@ -425,6 +448,7 @@
             pltpu.SemaphoreType.DMA((copies,)),
             pltpu.SemaphoreType.DMA((copies,)),
             pltpu.SemaphoreType.DMA((7,)),
+            pltpu.SemaphoreType.REGULAR((planes,)),
         ],
         compiler_params=pltpu.CompilerParams(
             collective_id=0, has_side_effects=True, vmem_limit_bytes=50 * 1024 * 1024

time: 41.3 us -> 39.2 us (0.949)
  Pallas kernels: 40.5 us -> 38.4 us
    pallas_call x1, Pallas kernels: 39.3 us -> 37.2 us  [fused_local(): pl.pallas_call(functools.partial(fused, planes, 1.0 / n), out_shape=shape...]
where the time goes in v1:
time: 39.2 us; the launch traced here: 39.1 us
  Pallas kernels  38.4 us (98%)
  between operations  0.64 us (2%)
    pallas_call x1, Pallas kernels, fused_local(): pl.pallas_call(functools.partial(fused, planes, 1.0 / n), out_shape=shape...  37.2 us
    pallas_call x1, Pallas kernels, fused_local(): pl.pallas_call(flush, out_shape=shapes, in_specs=[pl.BlockSpec(memory_spa...  1.27 us

profile of v1, /device:TPU:0, one launch (start us, length us, event | category | flops | bytes accessed | tf_op | source)
XLA Modules:
  0.0 39.1 jit_solution(8966527460326636524)
XLA Ops:
  0.6 37.2 %fused_sections.1 = (bf16[192,1024]{1,0:T(8,128)(2,1)S(1)}, bf16[192,1024]{1,0:T(8,128)(2,1)S(1)}, bf16[192,1024]{1,0:T(8,128)(2,1)S(1)}, bf16[192,1024]{1,0:T(8,128)(2,1)S(1)}, f32[64,1024]{1,0:T(8,128)S(1)}) custom-call(bf16[192,1024]{1,0:T(8,128)(2,1)} %bitcast.11, bf16[192,1024]{1,0:T(8,128)(2,1)} %bitcast.12, bf16[192,1024]{1,0:T(8,128)(2,1)} %bitcast.13, ...), custom_call_target="tpu_custom_call" | custom-call | tf_op jit(solution)/shard_map/fused_sections/pallas_call | solution.py:421
  37.8 1.3 %flush.1 = (bf16[192,1024]{1,0:T(8,128)(2,1)}, bf16[192,1024]{1,0:T(8,128)(2,1)}, bf16[192,1024]{1,0:T(8,128)(2,1)}, bf16[192,1024]{1,0:T(8,128)(2,1)}, f32[64,1024]{1,0:T(8,128)}) custom-call(bf16[192,1024]{1,0:T(8,128)(2,1)S(1)} %get-tuple-element.15.refs_0_, bf16[192,1024]{1,0:T(8,128)(2,1)S(1)} %get-tuple-element.16.refs_1_, ...), custom_call_target="tpu_custom_call" | custom-call | tf_op jit(solution)/shard_map/flush/pallas_call | solution.py:464

commit v2 on v1

--- a/solution.py
+++ b/solution.py
@@ -107,21 +107,24 @@
     planes, weight,
     q_in, k_in, v_in, w_in, ids_in, res_in, cot_in,
     out_ref, gq_ref, gk_ref, gv_ref, gp_ref,
-    wbuf, cotg, attg, transit, att_send, att_cols, att_rows, probs, bias, dbuf,
-    prod, rs_send, rs_recv, branch, running,
+    wbuf, cotg, attg, apair, att_send, att_cols, probs, bias, d_cols, d_send, d_recv,
+    prod, rs_send, rs_recv, branch, paired, b_send, b_recv, b_relay, running,
     q_ref, k_ref, v_ref, ids_ref, res_ref, cot_ref, send_sems, recv_sems, load_sems, above_sems,
+    rs_sems,
 ):
     length, inner = q_ref.shape
     res_width = cot_ref.shape[1]
     rows = w_in.shape[0]
     half, quarter = length // 2, length // 4
+    chunks = res_width // 256
     scale = HD ** (-0.5)
     sections = lax.axis_size("aa")
     a, b = lax.axis_index("aa"), lax.axis_index("ba")
     x, y, z = b % 2, (b // 2) % 2, b // 4
     q = b % 4
     xn, yn = b + 1 - 2 * x, b + 2 - 4 * y
-    qx, qy, qd = q + 1 - 2 * x, q + 2 - 4 * y, 3 - q
+    pn, gn = xn + a * (yn - xn), yn + a * (xn - yn)
+    qp, qg, qd = pn % 4, gn % 4, 3 - q
     zs = [flipped(z, k) for k in range(planes)]
 
     def there(dest, other=False):
@@ -130,7 +133,10 @@
     def rows_of(start, size, step):
         return pl.ds(pl.multiple_of(start, step), size)
 
-    w_ref = wbuf.at[rows_of(b * rows, rows, rows)]
+    def shard(slot, zk):
+        return wbuf.at[slot, rows_of(zk * rows, rows, rows)]
+
+    w_ref = shard(0, z)
     loads = [
         pltpu.make_async_copy(src, dst, load_sems.at[i])
         for i, (src, dst) in enumerate((
@@ -171,17 +177,12 @@
             device_id=device, device_id_type=pl.DeviceIdType.MESH,
         )
 
-    def shard(zk, qq, part=None):
-        start = (zk * 4 + qq) * rows
-        if part is None:
-            return wbuf.at[rows_of(start, rows, rows)]
-        return wbuf.at[rows_of(start + part * (rows // 2), rows // 2, rows // 2)]
-
     my_half = rows_of(a * half, half, quarter)
     part_a = rows_of(a * half, quarter, quarter)
     part_b = rows_of(a * half + quarter, quarter, quarter)
     other = there(b, True)
     to_x, to_y = there(xn), there(yn)
+    to_p, to_g = there(pn), there(gn)
 
     cot_x = remote(cot_ref.at[my_half], cotg.at[0, my_half], to_x)
     cot_y = remote(cot_ref.at[my_half], cotg.at[1, my_half], to_y)
@@ -190,32 +191,29 @@
     cot_da = remote(cotg.at[0, part_a], cotg.at[2, part_a], to_y)
     cot_db = remote(cotg.at[1, part_b], cotg.at[2, part_b], to_x)
     cot_do = remote(cotg.at[2, my_half], cotg.at[2, my_half], other)
-    w_z = [None] + [
-        remote(w_ref, shard(z, q), there(b + 4 * (zs[k] - z))) for k in range(1, planes)
-    ]
-    w_x, w_y, w_a, w_b = [], [], [], []
-    for k in range(planes):
-        mine = w_ref if k == 0 else shard(zs[k], q)
-        w_x.append(remote(mine, shard(zs[k], q), to_x))
-        w_y.append(remote(mine, shard(zs[k], q), to_y))
-        if k == 1:
-            w_d = remote(shard(z, qd), shard(z, qd), there(b + 4 * (zs[1] - z)))
-            w_a.append(w_d)
-            w_b.append(w_d)
-            continue
-        w_a.append(remote(shard(zs[k], qx, 0), shard(zs[k], qx, 0), to_y))
-        w_b.append(remote(shard(zs[k], qy, 1), shard(zs[k], qy, 1), to_x))
-    low, high = pl.ds(0, half), pl.ds(half, half)
-    att_x = remote(att_send.at[qx], attg.at[0], to_x)
-    att_y = remote(att_send.at[qy], attg.at[1], to_y)
-    att_ta = remote(att_send.at[qd, low], transit.at[0], to_x)
-    att_tb = remote(att_send.at[qd, high], transit.at[1], to_y)
-    att_fa = remote(transit.at[0], attg.at[2, low], to_y)
-    att_fb = remote(transit.at[1], attg.at[2, high], to_x)
-    rs_z = [None] + [
-        remote(
-            rs_send.at[rows_of(zs[k] * rows, rows, rows)], rs_recv.at[k - 1],
-            there(b + 4 * (zs[k] - z)),
+    w_z = [None] + [remote(w_ref, shard(0, z), columns[k]) for k in range(1, planes)]
+    w_g = [remote(shard(0, zs[k]), shard(1, zs[k]), to_g) for k in range(planes)]
+    att_p = remote(att_send.at[qp], attg.at[a], to_p)
+    att_d = remote(att_send.at[qd], apair, to_p)
+    att_g = remote(att_send.at[qg], attg.at[1 - a], to_g)
+    att_f = remote(apair, attg.at[2], to_g)
+    d_p = [remote(d_send.at[i], d_recv.at[i], to_p) for i in range(2)]
+    b_p = [remote(b_send.at[c], b_recv.at[c], to_p) for c in range(chunks)]
+    b_o = [remote(b_recv.at[c], b_relay.at[c], other) for c in range(chunks)]
+    rs_out = []
+    for dest in range(planes):
+        k = flipped(z, dest)
+        slot = jnp.maximum(k - 1, 0)
+        rs_out.append(pltpu.make_async_remote_copy(
+            src_ref=rs_send.at[pl.ds(dest * rows, rows)], dst_ref=rs_recv.at[slot],
+            send_sem=rs_sems.at[0, slot], recv_sem=rs_sems.at[1, slot],
+            device_id=there(b + 4 * (dest - z)), device_id_type=pl.DeviceIdType.MESH,
+        ))
+    rs_in = [
+        pltpu.make_async_remote_copy(
+            src_ref=rs_send.at[pl.ds(0, rows)], dst_ref=rs_recv.at[k - 1],
+            send_sem=rs_sems.at[0, k - 1], recv_sem=rs_sems.at[1, k - 1],
+            device_id=columns[k], device_id_type=pl.DeviceIdType.MESH,
         )
         for k in range(1, planes)
     ]
@@ -230,7 +228,6 @@
     loads[0].wait()
     go(cot_x, cot_y)
     loads[1].wait()
-    go(w_x[0], w_y[0])
 
     def to_planes(above):
         for k in range(1, planes):
@@ -270,7 +267,6 @@
         for h in range(4):
             att_cols[h, rows_of(zk * HD, HD, HD), :] = parts[h].astype(BF)
             probs[4 * zk + h] = shares[h]
-        att_rows[:, unit] = jnp.concatenate(parts, axis=0).T.astype(BF)
         return carry
 
     lax.fori_loop(0, planes // 2, forward, 0)
@@ -278,121 +274,162 @@
     lax.fori_loop(planes // 2, planes, forward, 0)
     for h in range(4):
         att_send[h] = turned(att_cols[h]).astype(BF)
+    go(att_d, att_p, att_g)
 
     cot_x.wait_recv()
     cot_y.wait_recv()
     go(cot_xo, cot_yo)
-    go(att_ta, att_tb, att_x, att_y)
     go(cot_da, cot_db)
 
-    def pass_planes(k):
+    def pass_plane(k):
         w_z[k].wait_recv()
-        go(w_x[k], w_y[k])
-
-    def pass_diagonal(k):
-        w_x[k].wait_recv()
-        w_y[k].wait_recv()
-        if k != 1:
-            go(w_a[k], w_b[k])
-
-    def backward(k, first):
-        unit = rows_of(zs[k] * width, width, width)
-        dbuf[...] = nt(cot_ref[...], wbuf[unit, :]).astype(BF)
-        mine = att_rows[:, unit]
-
-        def add(c, carry):
-            tile = rows_of(c * 256, 256, 256)
-            term = mm(mine, wbuf[unit, tile])
-            branch[:, tile] = term if first else branch[:, tile] + term
-            return carry
-
-        lax.fori_loop(0, res_width // 256, add, 0, unroll=True)
-
-    def grads(k):
-        unit = rows_of(zs[k] * width, width, width)
-        d4, q4, v4 = dbuf[...], q_ref[:, unit], v_ref[:, unit]
+        go(w_g[k])
+
+    def near(c, carry):
+        tile = rows_of(c * 256, 256, 256)
+        total = mm(att_cols[q], cot_ref[:, tile])
+        for i in range(2):
+            total = total + mm(flat[i], cotg[i, :, tile])
+        prod[:, tile] = total
+        return carry
+
+    def far(c, carry):
+        tile = rows_of(c * 256, 256, 256)
+        total = (prod[:, tile] + mm(flat[2], cotg[2, :, tile])) * weight
+        prod[:, tile] = total
+        rs_send[:, tile] = total.astype(BF)
+        return carry
+
+    def backward(i):
+        block, mine, theirs = wbuf.at[i], att_send[(q, qg)[i]], (attg.at[a], apair)[i][...]
+        d_send[i] = nt(cotg[a], block[...]).astype(BF)
+        go(d_p[i])
+        for c in range(chunks):
+            tile = slice(c * 256, (c + 1) * 256)
+            term = mm(theirs, block[:, tile])
+            if i == 0:
+                paired[:, tile] = term
+            else:
+                b_send[c] = (paired[:, tile] + term).astype(BF)
+                go(b_p[c])
+        for c in range(chunks):
+            tile = slice(c * 256, (c + 1) * 256)
+            term = mm(mine, block[:, tile])
+            branch[:, tile] = term if i == 0 else branch[:, tile] + term
+        d_cols[(q, qg)[i]] = nt(block[...], cot_ref[...]).astype(BF)
+
+    def grads(zk):
+        unit = rows_of(zk * width, width, width)
+        rows_in = rows_of(zk * HD, HD, HD)
+        q4, v4 = q_ref[:, unit], v_ref[:, unit]
         k_turned = turned(k_ref[:, unit]).astype(BF)
         spans = [slice(h // 2 * PAIR, (h // 2 + 1) * PAIR) for h in range(4)]
-        d_probs = [nt(v4[:, spans[h]] * ones[h % 2], d4[:, spans[h]]) for h in range(4)]
+        d_pairs = [
+            jnp.concatenate([d_cols[2 * i, rows_in, :], d_cols[2 * i + 1, rows_in, :]], axis=0)
+            for i in range(2)
+        ]
+        d_probs = [mm(v4[:, spans[h]] * ones[h % 2], d_pairs[h // 2]) for h in range(4)]
         d_scores, low = [], []
         for h in range(4):
-            share = probs[4 * zs[k] + h]
+            share = probs[4 * zk + h]
             delta = jnp.sum(share * d_probs[h], axis=0, keepdims=True)
             d_scores.append((share * (d_probs[h] - delta)).astype(BF))
             low.append(share.astype(BF))
-        gv = [mm(low[h], d4[:, spans[h]] * ones[h % 2]) for h in range(4)]
+        gv = [nt(low[h], d_pairs[h // 2]) for h in range(4)]
         gk = [mm(d_scores[h], q4[:, spans[h]] * scaled[h % 2]) for h in range(4)]
         gq = [mm(k_turned[h * HD:(h + 1) * HD], d_scores[h]) for h in range(4)]
-        gv_ref[:, unit] = jnp.concatenate([gv[0] + gv[1], gv[2] + gv[3]], axis=1).astype(BF)
+        left = lane < HD
+        gv = [jnp.where(left, gv[2 * i], gv[2 * i + 1]) for i in range(2)]
+        gv_ref[:, unit] = jnp.concatenate(gv, axis=1).astype(BF)
         gk_ref[:, unit] = jnp.concatenate([gk[0] + gk[1], gk[2] + gk[3]], axis=1).astype(BF)
         gq_ref[:, unit] = (jnp.concatenate(gq, axis=0) * scale).T.astype(BF)
 
-    def last_piece(k):
-        w_a[k].wait_recv()
-        if k != 1:
-            w_b[k].wait_recv()
-        if k == 0:
-            go(w_d)
-
-    att_ta.wait_recv()
-    att_tb.wait_recv()
-    go(att_fa, att_fb)
-    pass_diagonal(0)
-    pass_planes(1)
+    def later_planes():
+        for k in range(2, planes):
+            pass_plane(k)
+        backward(0)
+
+    att_d.wait_recv()
+    go(att_f)
+    go(w_g[0])
+    pass_plane(1)
+    for copy in (cot_xo, cot_yo, att_p, att_g):
+        copy.wait_recv()
+    flat = [turned(attg[i]).astype(BF) for i in range(2)]
+    lax.fori_loop(0, chunks, near, 0)
     cot_da.wait_recv()
     cot_db.wait_recv()
     go(cot_do)
-    for k in range(2, planes):
-        pass_planes(k)
-    last_piece(0)
-    backward(0, True)
-    for copy in (cot_xo, cot_yo, cot_do, att_x, att_y, att_fa, att_fb):
-        copy.wait_recv()
-
-    flat = [turned(attg[i]).astype(BF) for i in range(3)]
-
-    def product(c, carry):
-        tile = rows_of(c * 256, 256, 256)
-        total = mm(att_cols[q], cot_ref[:, tile])
-        for i in range(3):
-            total = total + mm(flat[i], cotg[i, :, tile])
-        total = total * weight
-        prod[:, tile] = total
-        rs_send[:, tile] = total.astype(BF)
+    count_started = len(started)
+
+    @pl.when(z >= planes // 2)
+    def _():
+        later_planes()
+
+    del started[count_started:]
+    cot_do.wait_recv()
+    att_f.wait_recv()
+    flat.append(turned(attg[2]).astype(BF))
+    lax.fori_loop(0, chunks, far, 0)
+    for dest in range(planes):
+        @pl.when(dest != z)
+        def _(dest=dest):
+            rs_out[dest].start()
+
+    @pl.when(z < planes // 2)
+    def _():
+        later_planes()
+
+    d_p[0].wait_recv()
+    d_cols[qp] = turned(d_recv[0]).astype(BF)
+    for k in range(planes):
+        w_g[k].wait_recv()
+    backward(1)
+
+    @pl.when(a == 0)
+    def _():
+        relay.start()
+
+    d_p[1].wait_recv()
+    d_cols[qd] = turned(d_recv[1]).astype(BF)
+
+    def grads_step(zk, carry):
+        grads(zk)
         return carry
 
-    lax.fori_loop(0, res_width // 256, product, 0)
-    pass_diagonal(1)
-    go(*rs_z[:0:-1])
-    grads(0)
-    for k in range(1, planes):
-        if k + 1 < planes:
-            pass_diagonal(k + 1)
-        last_piece(k)
-        backward(k, False)
-        if k == planes - 1:
-            @pl.when(a == 0)
-            def _():
-                relay.start()
-        grads(k)
+    lax.fori_loop(0, planes, grads_step, 0)
     total = prod[rows_of(z * rows, rows, rows), :]
     for k in range(1, planes):
-        rs_z[k].wait_recv()
+        rs_in[k - 1].wait_recv()
         total = total + rs_recv[k - 1].astype(F32)
     gp_ref[...] = total
-    base = res_ref[...].astype(F32) + branch[...]
-
-    @pl.when(a == 0)
-    def _():
-        out_ref[...] = base.astype(BF)
-        relay.wait_send()
 
     @pl.when(a == 1)
     def _():
         relay.wait_recv()
-        out_ref[...] = (base + running[...]).astype(BF)
-
-    for copy in started:
+
+    for c in range(chunks):
+        tile = slice(c * 256, (c + 1) * 256)
+        b_p[c].wait_recv()
+        base = res_ref[:, tile].astype(F32) + branch[:, tile] + b_recv[c].astype(F32)
+
+        @pl.when(a == 0)
+        def _(c=c, tile=tile, base=base):
+            b_o[c].start()
+            out_ref[:, tile] = base.astype(BF)
+
+        @pl.when(a == 1)
+        def _(c=c, tile=tile, base=base):
+            b_o[c].wait_recv()
+            out_ref[:, tile] = (base + running[:, tile] + b_relay[c].astype(F32)).astype(BF)
+
+    @pl.when(a == 0)
+    def _():
+        relay.wait_send()
+        for copy in b_o:
+            copy.wait_send()
+
+    for copy in started + rs_in:
         copy.wait_send()
 
 
@@ -411,7 +448,8 @@
     res_width = residual_in.shape[2]
     rows = out_proj.shape[1]
     planes = n // 4
-    copies = 7 + (planes - 1) + 4 * planes + 6 + (planes - 1) + 1
+    chunks = res_width // 256
+    copies = 7 + (planes - 1) + planes + 4 + 2 + 2 * chunks + 1
     heads = inner // HD
     wide = jax.ShapeDtypeStruct((length, inner), BF)
     shapes = [
@@ -424,20 +462,25 @@
         in_specs=[pl.BlockSpec(memory_space=pltpu.HBM)] * 7,
         out_specs=[pl.BlockSpec(memory_space=pltpu.VMEM)] * 5,
         scratch_shapes=[
-            pltpu.VMEM((inner, res_width), BF),
+            pltpu.VMEM((2, planes * rows, res_width), BF),
             pltpu.VMEM((3, length, res_width), BF),
             pltpu.VMEM((3, length, planes * rows), BF),
-            pltpu.VMEM((2, length // 2, planes * rows), BF),
+            pltpu.VMEM((length, planes * rows), BF),
             pltpu.VMEM((4, length, planes * rows), BF),
             pltpu.VMEM((4, planes * rows, length), BF),
-            pltpu.VMEM((length, inner), BF),
             pltpu.VMEM((heads, length, length), F32),
             pltpu.VMEM((length, length), F32),
-            pltpu.VMEM((length, 4 * HD), BF),
+            pltpu.VMEM((4, planes * rows, length), BF),
+            pltpu.VMEM((2, length, planes * rows), BF),
+            pltpu.VMEM((2, length, planes * rows), BF),
             pltpu.VMEM((planes * rows, res_width), F32),
             pltpu.VMEM((planes * rows, res_width), BF),
             pltpu.VMEM((planes - 1, rows, res_width), BF),
             pltpu.VMEM((length, res_width), F32),
+            pltpu.VMEM((length, res_width), F32),
+            pltpu.VMEM((chunks, length, 256), BF),
+            pltpu.VMEM((chunks, length, 256), BF),
+            pltpu.VMEM((chunks, length, 256), BF),
             pltpu.VMEM((length, res_width), F32),
             pltpu.VMEM((length, inner), BF),
             pltpu.VMEM((length, inner), BF),
@@ -449,6 +492,7 @@
             pltpu.SemaphoreType.DMA((copies,)),
             pltpu.SemaphoreType.DMA((7,)),
             pltpu.SemaphoreType.REGULAR((planes,)),
+            pltpu.SemaphoreType.DMA((2, planes - 1)),
         ],
         compiler_params=pltpu.CompilerParams(
             collective_id=0, has_side_effects=True, vmem_limit_bytes=50 * 1024 * 1024

time: 39.2 us -> 36.7 us (0.936)
  Pallas kernels: 38.4 us -> 35.9 us
    pallas_call x1, Pallas kernels: 37.2 us -> 34.7 us  [fused_local(): pl.pallas_call(functools.partial(fused, planes, 1.0 / n), out_shape=shape...]
where the time goes in v2:
time: 36.7 us; the launch traced here: 36.6 us
  Pallas kernels  35.9 us (98%)
  between operations  0.64 us (2%)
    pallas_call x1, Pallas kernels, fused_local(): pl.pallas_call(functools.partial(fused, planes, 1.0 / n), out_shape=shape...  34.7 us
    pallas_call x1, Pallas kernels, fused_local(): pl.pallas_call(flush, out_shape=shapes, in_specs=[pl.BlockSpec(memory_spa...  1.27 us

profile of v2, /device:TPU:0, one launch (start us, length us, event | category | flops | bytes accessed | tf_op | source)
XLA Modules:
  0.0 36.6 jit_solution(16867089484594013813)
XLA Ops:
  0.6 34.7 %fused_sections.1 = (bf16[192,1024]{1,0:T(8,128)(2,1)S(1)}, bf16[192,1024]{1,0:T(8,128)(2,1)S(1)}, bf16[192,1024]{1,0:T(8,128)(2,1)S(1)}, bf16[192,1024]{1,0:T(8,128)(2,1)S(1)}, f32[64,1024]{1,0:T(8,128)S(1)}) custom-call(bf16[192,1024]{1,0:T(8,128)(2,1)} %bitcast.11, bf16[192,1024]{1,0:T(8,128)(2,1)} %bitcast.12, bf16[192,1024]{1,0:T(8,128)(2,1)} %bitcast.13, ...), custom_call_target="tpu_custom_call" | custom-call | tf_op jit(solution)/shard_map/fused_sections/pallas_call | solution.py:459
  35.3 1.3 %flush.1 = (bf16[192,1024]{1,0:T(8,128)(2,1)}, bf16[192,1024]{1,0:T(8,128)(2,1)}, bf16[192,1024]{1,0:T(8,128)(2,1)}, bf16[192,1024]{1,0:T(8,128)(2,1)}, f32[64,1024]{1,0:T(8,128)}) custom-call(bf16[192,1024]{1,0:T(8,128)(2,1)S(1)} %get-tuple-element.15.refs_0_, bf16[192,1024]{1,0:T(8,128)(2,1)S(1)} %get-tuple-element.16.refs_1_, ...), custom_call_target="tpu_custom_call" | custom-call | tf_op jit(solution)/shard_map/flush/pallas_call | solution.py:508
